TPU v7x, 32 devices: a whole 2x2x4 slice. The times are simulated.
32 devices in a mesh: wave: 8 (over y, x, core), lev: 4 (over z).
Axes of the slice: x: 2, y: 2, z: 4, core: 2. Of those that a mesh axis runs over, the one named last changes fastest.
Arguments:
- spec: bfloat16 [16, 128, 640], P('wave', 'lev'), may hold values from -1.5 to 1.5
- legendre: bfloat16 [16, 1280, 640], P('wave'), may hold values from -0.25 to 0.25
- layer_depth_share: float32 [16], P('lev'), may hold values from 0.5 to 2
- quad_weight: float32 [1280], replicated, may hold values from 8 to 32
- wave_of_slot: int32 [16], P('wave'), may hold values from 0 to 639, as said below
Outputs:
- tendency: bfloat16 [16, 128, 640], P('wave', 'lev')
Inputs may be any that keep to these rules, and one draw needn't show every extreme that they name: `wave_of_slot`: slots 2 i and 2 i + 1 hold wavenumbers m and 639 - m; no wavenumber appears twice.
All inputs are finite; a program needn't handle non-finite values.
Results may differ from a plain program's by a relative error of at most 0.0047.
The roundings to bfloat16 on the way count: a program that leaves them out, or rounds other values in their place, can miss the bound.
Values may be sent and summed in bfloat16 or wider, within the bound.
A program may use at most 128 MiB of HBM per device.

v0:
```python
import functools
import math

import jax
import jax.numpy as jnp
import numpy as np
from jax import lax
from jax.experimental import pallas as pl
from jax.experimental.pallas import tpu as pltpu
from jax.sharding import PartitionSpec as P

LANES = 128
POINTS = 2 * LANES
UNROLL = 4
NT = (((1,), (1,)), ((), ()))


def taylor(first, count):
    return [(-1.0) ** k / math.factorial(2 * k + first) for k in range(count)]


def horner(square, terms):
    total = jnp.full_like(square, terms[-1])
    for term in reversed(terms[:-1]):
        total = total * square + term
    return total


def turn_trig(steps, length, inverse):
    whole = jnp.floor(steps * inverse + 0.5)
    angle = (steps - whole * length) * inverse * (2.0 * math.pi)
    square = angle * angle
    return horner(square, taylor(0, 10)), angle * horner(square, taylor(1, 10))


def lane_maps(slots, fields, layers):
    order = np.arange(slots * 2 * 2 * fields * layers)
    natural = order.reshape(slots, 2, 2, fields, layers)
    return natural.transpose(0, 2, 3, 1, 4).reshape(-1)


def fourier_stage(dims, spec_ref, leg_ref, loads, live, gain, perm_ref, rows_ref):
    slots, columns, half = dims["slots"], dims["columns"], dims["half"]
    total = jnp.zeros((half, LANES), jnp.float32)
    for slot in range(slots):
        masked = spec_ref[slot] * live[slot].astype(jnp.bfloat16)
        for hemi in range(2):
            at = (slot * 2 + hemi) * columns
            pieces = []
            if at:
                pieces.append(jnp.zeros((at, masked.shape[1]), masked.dtype))
            pieces.append(masked)
            if at + columns < LANES:
                pieces.append(jnp.zeros((LANES - at - columns, masked.shape[1]), masked.dtype))
            loads[slot * 2 + hemi].wait()
            total += lax.dot_general(
                leg_ref[slot, hemi * half : (hemi + 1) * half, :],
                jnp.concatenate(pieces, 0),
                NT,
                preferred_element_type=jnp.float32,
            )
    rows = jnp.dot(total.astype(jnp.bfloat16), perm_ref[...], preferred_element_type=jnp.float32)
    rows_ref[...] = rows * gain


def split_rows(dims, rows_ref, send_ref):
    quarter, half = dims["quarter"], dims["half"]
    for place in range(dims["groups"]):
        low = rows_ref[place * quarter : (place + 1) * quarter, :]
        top = half - place * quarter
        high = rows_ref[top - quarter : top, :]
        send_ref[place] = jnp.concatenate([low, high], 0).astype(jnp.bfloat16)


def whereabouts(dims, device, number):
    quarter, block = dims["quarter"], dims["block"]
    local = [number * block + u for u in range(block)]
    dist = [
        jnp.where(
            r < quarter, device * quarter + r, dims["half"] - (device + 2) * quarter + r
        )
        for r in local
    ]
    lengths = [20 + 4 * q for q in dist]
    return local, dist, lengths, [length.astype(jnp.float32) for length in lengths]


def tiles_of(longest):
    return (longest // 2 + POINTS) // POINTS


def most_tiles(dims):
    quarter, block, half = dims["quarter"], dims["block"], dims["half"]
    most = 0
    for device in range(dims["groups"]):
        total = 0
        for number in range(2 * quarter // block):
            r = number * block + block - 1
            q = device * quarter + r if r < quarter else half - (device + 2) * quarter + r
            total += tiles_of(20 + 4 * q)
        most = max(most, total)
    return most


def back_home(dims, part, slot, u):
    width = 2 * dims["waves"]
    if width >= LANES:
        return u * width + part * dims["waves"] + slot * dims["groups"]
    share = LANES // width
    inner = (part * dims["slots"] + slot) * share + u % share
    return u // share * LANES + inner * dims["groups"]


def table_stage(dims, device, waves, quad_ref, cor_ref, scratch):
    slots, groups, half = dims["slots"], dims["groups"], dims["half"]
    fields, layers, block = dims["fields"], dims["layers"], dims["block"]
    state, hop, tab, back_tab, cor, scale = scratch
    total_lat = 2 * half
    pair = min(2, block)
    wide = slots * block * groups
    lane = lax.broadcasted_iota(jnp.int32, (groups, LANES), 1).astype(jnp.float32)
    north_row = lax.broadcasted_iota(jnp.int32, (2 * layers, LANES), 0) < layers
    wave_row = lax.broadcasted_iota(jnp.int32, (2 * layers, POINTS), 0) < layers
    width = 2 * dims["waves"]
    column = lax.broadcasted_iota(jnp.int32, (2 * layers, POINTS), 1)
    if width >= LANES:
        owner = column // width
    else:
        share = LANES // width
        owner = column // LANES * share + column // groups % share

    def group(number, first):
        local, dist, lengths, floats = whereabouts(dims, device, number)
        scaled = jnp.zeros((2 * layers, POINTS), jnp.float32)
        for u, length in enumerate(floats):
            inverse = 1.0 / jnp.full((groups, LANES), length, jnp.float32)
            for slot in range(slots):
                begin = turn_trig(waves[slot] * lane, length, inverse)
                cosine = jnp.broadcast_to(begin[0][:, LANES // 2 : LANES // 2 + 1], (groups, LANES))
                sine = jnp.broadcast_to(begin[1][:, LANES // 2 : LANES // 2 + 1], (groups, LANES))
                keep = jnp.where(2.0 * waves[slot] < length, 1.0, 0.0)
                at = (slot * block + u) * groups
                state[0, at : at + groups, :] = begin[0] * keep
                state[1, at : at + groups, :] = begin[1] * keep
                hop[0, at : at + groups, :] = cosine * cosine - sine * sine
                hop[1, at : at + groups, :] = 2.0 * cosine * sine
            cor[number, u * 2 * layers : (u + 1) * 2 * layers, :] = jnp.where(
                north_row, cor_ref[dist[u]], cor_ref[total_lat - 1 - dist[u]]
            )
            here = jnp.where(wave_row, quad_ref[dist[u]], quad_ref[total_lat - 1 - dist[u]])
            scaled = jnp.where(owner == u, here / length, scaled)
        scale[number] = scaled

        def tile(index, item):
            for side in range(POINTS // LANES):
                cols = slice(side * LANES, (side + 1) * LANES)
                point = lane + (index * POINTS + side * LANES).astype(jnp.float32)
                start = jnp.minimum(point + 0.5, 1.0)
                weight = [
                    jnp.maximum(jnp.minimum(0.5 * length + 0.5 - point, start), 0.0)
                    for length in floats
                ]
                for u in range(0, block, pair):
                    both = jnp.concatenate(weight[u : u + pair], 0).astype(jnp.bfloat16)
                    for slot in range(slots):
                        at = (slot * block + u) * groups
                        rows = slice(at, at + pair * groups)
                        cosine, sine = state[0, rows, :], state[1, rows, :]
                        turn_cos, turn_sin = hop[0, rows, :], hop[1, rows, :]
                        state[0, rows, :] = cosine * turn_cos - sine * turn_sin
                        state[1, rows, :] = sine * turn_cos + cosine * turn_sin
                        for part, value in enumerate((cosine, sine)):
                            packed = value.astype(jnp.bfloat16)
                            put = part * wide + at
                            tab[item, put : put + pair * groups, cols] = packed
                            put = back_home(dims, part, slot, u)
                            back_tab[item, put : put + pair * groups, cols] = packed * both
            return item + 1

        return lax.fori_loop(0, tiles_of(lengths[-1]), tile, first)

    lax.fori_loop(0, 2 * dims["quarter"] // block, group, 0)


def coefficient_stage(dims, get_ref, base, total):
    slots, groups, layers = dims["slots"], dims["groups"], dims["layers"]
    fields, block, count = dims["fields"], dims["block"], 2 * dims["quarter"]
    width = fields * 2 * layers
    number = count // block
    lane = lax.broadcasted_iota(jnp.int32, (groups, LANES), 1)
    south_lane = lane // layers % 2 == 1
    first_slot = lax.broadcasted_iota(jnp.int32, (width, LANES), 1) < block * groups
    eye = (
        lax.broadcasted_iota(jnp.int32, (LANES, LANES), 0)
        == lax.broadcasted_iota(jnp.int32, (LANES, LANES), 1)
    ).astype(jnp.bfloat16)
    for start in range(0, number, 2):
        pieces = []
        for n in range(start, min(start + 2, number)):
            both = []
            for u in range(block):
                at = n * block + u
                north = get_ref[pl.ds(at, groups, stride=count), :]
                south = get_ref[pl.ds(count - 1 - at, groups, stride=count), :]
                both.append(jnp.where(south_lane, south, north))
            pieces += both * (LANES // (block * groups))
        turned = lax.dot_general(
            eye,
            jnp.concatenate(pieces, 0).astype(jnp.bfloat16),
            NT,
            preferred_element_type=jnp.float32,
        )
        for n in range(start, min(start + 2, number)):
            mine = turned[:, (n - start) * LANES : (n - start + 1) * LANES]
            for part in range(2):
                value = [
                    mine[(slot * 2 + part) * width : (slot * 2 + part + 1) * width]
                    for slot in range(slots)
                ]
                base[n, :, part * LANES : (part + 1) * LANES] = jnp.where(
                    first_slot, value[0], value[1]
                ).astype(jnp.bfloat16)
    total[...] = jnp.zeros_like(total)


def item_stage(dims, device, base, tab, back_tab, cor, total):
    groups, layers, block = dims["groups"], dims["layers"], dims["block"]
    fields, number = dims["fields"], 2 * dims["quarter"] // dims["block"]
    width = fields * 2 * layers
    rows = 2 * width
    ends = []
    for n in range(number):
        lengths = whereabouts(dims, device, n)[2]
        ends.append(tiles_of(lengths[-1]) + (ends[-1] if ends else 0))
    lane = lax.broadcasted_iota(jnp.int32, (width, LANES), 1)
    mine = [
        (lane // groups % block == u).astype(jnp.float32).astype(jnp.bfloat16)
        for u in range(block)
    ]
    span = 2 * dims["waves"]
    share = max(1, LANES // span)
    reach = max(LANES, span)
    across = lax.broadcasted_iota(jnp.int32, (width, reach), 1)
    sign = jnp.where(across // (reach // 2) == 0, 1.0, -1.0)

    def one(item):
        n = 0
        for end in ends:
            n = n + jnp.where(item >= end, 1, 0)
        real = base[n, :, :LANES]
        imag = base[n, :, LANES:]
        pieces = []
        for u in range(block):
            left, right = real * mine[u], imag * mine[u]
            pieces.append(jnp.concatenate([left, -right], 1))
            pieces.append(jnp.concatenate([left, right], 1))
        grid = jnp.dot(
            jnp.concatenate(pieces, 0), tab[item], preferred_element_type=jnp.float32
        )
        made = []
        for u in range(block):
            extra = cor[n, u * 2 * layers : (u + 1) * 2 * layers, :]
            extra = jnp.concatenate([extra] * (POINTS // LANES), 1)
            for side in range(2):
                at = (u * 2 + side) * width
                part = [
                    grid[at + f * 2 * layers : at + (f + 1) * 2 * layers] for f in range(fields)
                ]
                absolute = part[2] + extra
                made += [
                    absolute * part[0],
                    absolute * part[1],
                    0.5 * (part[0] * part[0] + part[1] * part[1]),
                    part[0] * part[3],
                ]
        products = jnp.concatenate(made, 0).astype(jnp.bfloat16)
        back = lax.dot_general(
            products, back_tab[item], NT, preferred_element_type=jnp.float32
        )
        for start in range(0, block, share):
            column = start * span // LANES * LANES
            joined = jnp.zeros((width, reach), jnp.float32)
            for u in range(start, min(start + share, block)):
                near = back[u * rows : u * rows + width, column : column + reach]
                far = back[u * rows + width : (u + 1) * rows, column : column + reach]
                value = near * sign + far
                keep = across // groups % share == u - start
                joined = value if share == 1 else jnp.where(keep, value, joined)
            total[n, :, column : column + reach] += joined

    def body(step, carry):
        for k in range(UNROLL):
            one(step * UNROLL + k)
        return carry

    lax.fori_loop(0, (ends[-1] + UNROLL - 1) // UNROLL, body, 0)


def return_stage(dims, total, scale, put_refs):
    slots, groups, layers = dims["slots"], dims["groups"], dims["layers"]
    fields, block, count = dims["fields"], dims["block"], 2 * dims["quarter"]
    width, span = fields * 2 * layers, 2 * dims["waves"]
    number = count // block
    share = max(1, LANES // span)
    lane = lax.broadcasted_iota(jnp.int32, (block * groups, POINTS), 1)
    row = lax.broadcasted_iota(jnp.int32, (block * groups, POINTS), 0)
    if span >= LANES:
        owner, kind = lane // span, lane % span // groups
    else:
        owner = lane // LANES * share + lane // groups % share
        kind = lane % LANES // (groups * share)
    pick = (owner * groups + lane % groups == row).astype(jnp.float32).astype(jnp.bfloat16)
    keep = []
    for slot in range(slots):
        for part in range(2):
            at = (kind[:1] == part * slots + slot).astype(jnp.float32)
            keep.append(jnp.broadcast_to(at, (width, POINTS)).astype(jnp.bfloat16))
    for start in range(0, number, 2):
        pieces = []
        for n in range(start, min(start + 2, number)):
            value = total[n] * jnp.concatenate([scale[n]] * fields, 0)
            value = value.astype(jnp.bfloat16)
            pieces += [value * here for here in keep]
        turned = lax.dot_general(
            pick, jnp.concatenate(pieces, 0), NT, preferred_element_type=jnp.float32
        )
        for n in range(start, min(start + 2, number)):
            for u in range(block):
                at = n * block + u
                value = turned[
                    u * groups : (u + 1) * groups, (n - start) * LANES : (n - start + 1) * LANES
                ]
                put_refs[0][pl.ds(at, groups, stride=count), :] = value
                put_refs[1][pl.ds(count - 1 - at, groups, stride=count), :] = value


def grid_scratch(dims):
    slots, groups, block = dims["slots"], dims["groups"], dims["block"]
    layers, fields = dims["layers"], dims["fields"]
    number = 2 * dims["quarter"] // block
    wide = slots * block * groups
    items = -(-most_tiles(dims) // UNROLL) * UNROLL
    width = fields * 2 * layers
    return [
        pltpu.VMEM((2, wide, LANES), jnp.float32),
        pltpu.VMEM((2, wide, LANES), jnp.float32),
        pltpu.VMEM((items, 2 * wide, POINTS), jnp.bfloat16),
        pltpu.VMEM((items, 2 * wide, POINTS), jnp.bfloat16),
        pltpu.VMEM((number + 1, block * 2 * layers, LANES), jnp.float32),
        pltpu.VMEM((number, 2 * layers, POINTS), jnp.float32),
        pltpu.VMEM((number + 1, width, 2 * wide), jnp.bfloat16),
        pltpu.VMEM((number + 1, width, 2 * wide), jnp.float32),
    ]


def final_stage(dims, get, leg_ref, perm_ref):
    slots, columns, half = dims["slots"], dims["columns"], dims["half"]
    turned = lax.dot_general(
        perm_ref[...], get, NT, preferred_element_type=jnp.float32
    ).astype(jnp.bfloat16)
    results = []
    for slot in range(slots):
        total = 0.0
        for hemi in range(2):
            at = (slot * 2 + hemi) * columns
            total += jnp.dot(
                turned[at : at + columns],
                leg_ref[slot, hemi * half : (hemi + 1) * half, :],
                preferred_element_type=jnp.float32,
            )
        results.append(total)
    return results


def joined_rows(dims, back_ref):
    quarter, groups = dims["quarter"], dims["groups"]
    low = [back_ref[place][:quarter] for place in range(groups)]
    high = [back_ref[place][quarter:] for place in reversed(range(groups))]
    return low + high


def to_peer(axis, shift):
    place = lax.axis_index(axis)
    count = lax.axis_size(axis)
    return {axis: lax.rem(place + shift, count)}


def exchange(axis, source_of, target_of, sems):
    place = lax.axis_index(axis)
    count = lax.axis_size(axis)
    copies = []
    for shift in range(1, count):
        peer = lax.rem(place + shift, count)
        copies.append(
            pltpu.make_async_remote_copy(
                src_ref=source_of(peer),
                dst_ref=target_of(place),
                send_sem=sems[0].at[shift],
                recv_sem=sems[1].at[shift],
                device_id=to_peer(axis, shift),
                device_id_type=pl.DeviceIdType.MESH,
            )
        )
    return copies


def whole_kernel(
    dims, spec_ref, leg_hbm, perm_ref, share_ref, quad_ref, cor_ref, wave_ref, out_ref,
    leg, rows, send, recv, back_send, back, wave_send, wave_recv, sum_send, sum_recv, geo,
    get, north, south, load_sem, sem_a, sem_b, sem_c, sem_d, sem_e, sem_f, sem_g, sem_h, *scratch,
):
    slots, groups, half = dims["slots"], dims["groups"], dims["half"]
    fields, layers, count = dims["fields"], dims["layers"], 2 * dims["quarter"]
    degrees = spec_ref.shape[2]
    me = lax.axis_index("wave")
    floor = lax.axis_index("lev")
    floors = lax.axis_size("lev")
    loads = []
    for slot in range(slots):
        for hemi in range(2):
            piece = pl.ds(hemi * half, half)
            copy = pltpu.make_async_copy(
                leg_hbm.at[slot, piece], leg.at[slot, piece], load_sem.at[slot * 2 + hemi]
            )
            copy.start()
            loads.append(copy)
    barrier = pltpu.get_barrier_semaphore()
    for axis, size in (("wave", groups), ("lev", floors)):
        for shift in range(1, size):
            pl.semaphore_signal(
                barrier, inc=1, device_id=to_peer(axis, shift), device_id_type=pl.DeviceIdType.MESH
            )
    degree = lax.broadcasted_iota(jnp.int32, (1, degrees), 1)
    live = [
        jnp.where(degree < degrees - wave_ref[slot], 1.0, 0.0).astype(jnp.float32)
        for slot in range(slots)
    ]
    row = lax.broadcasted_iota(jnp.int32, (8, LANES), 0)
    own = jnp.zeros((8, LANES), jnp.float32)
    for slot in range(slots):
        own = jnp.where(row == slot, wave_ref[slot].astype(jnp.float32), own)
    wave_send[...] = own
    geo[...] = jnp.zeros_like(geo)
    for slot in range(slots):
        full = spec_ref[slot].astype(jnp.float32) * live[slot]
        for part in range(2):
            first = part * fields * layers
            total = jnp.zeros((1, degrees), jnp.float32)
            for layer in reversed(range(layers)):
                at = first + 3 * layers + layer
                total = total + full[at : at + 1] * share_ref[layer]
                at = first + 2 * layers + layer
                geo[slot, at : at + 1, :] = total
            at = slot * 2 + part
            sum_send[at : at + 1, :] = total
    place = lax.broadcasted_iota(jnp.int32, (1, LANES), 1) // (LANES // slots)
    gain = jnp.ones((1, LANES), jnp.float32)
    for slot in range(slots):
        twice = jnp.where(wave_ref[slot] == 0, 1.0, 2.0)
        gain = jnp.where(place == slot, twice, gain)
    fourier_stage(dims, spec_ref, leg, loads, live, gain, perm_ref, rows)
    split_rows(dims, rows, send)
    pl.semaphore_wait(barrier, groups - 1 + floors - 1)

    def wave_place(device):
        return wave_recv.at[pl.ds(pl.multiple_of(device * 8, 8), 8)]

    tell = exchange("wave", lambda _: wave_send, wave_place, (sem_a, sem_b))
    lift = exchange("lev", lambda _: sum_send, lambda p: sum_recv.at[p], (sem_c, sem_d))
    for copy in tell:
        copy.start()
    wave_recv[pl.ds(pl.multiple_of(me * 8, 8), 8), :] = own
    there = exchange("wave", lambda p: send.at[p], lambda p: recv.at[p], (sem_e, sem_f))
    for copy in there + lift:
        copy.start()
    recv[me] = send[me]
    for copy in tell:
        copy.wait()
    waves = [wave_recv[pl.ds(slot, groups, stride=8), :] for slot in range(slots)]
    state, hop, tab, back_tab, cor, scale, base, total = scratch
    table_stage(dims, me, waves, quad_ref, cor_ref, scratch[:6])
    for copy in there:
        copy.wait()
    for source in range(groups):
        get[source * count : (source + 1) * count, :] = recv[source].astype(jnp.float32)
    coefficient_stage(dims, get, base, total)
    item_stage(dims, me, base, tab, back_tab, cor, total)
    return_stage(dims, total, scale, (north, south))
    hemi = lax.broadcasted_iota(jnp.int32, (count, LANES), 1) // layers % 2
    for source in range(groups):
        piece = slice(source * count, (source + 1) * count)
        back_send[source] = jnp.where(hemi == 1, south[piece], north[piece]).astype(jnp.bfloat16)
    home = exchange("wave", lambda p: back_send.at[p], lambda p: back.at[p], (sem_g, sem_h))
    for copy in home:
        copy.start()
    back[me] = back_send[me]
    for copy in lift:
        copy.wait()
    for slot in range(slots):
        for part in range(2):
            at = slot * 2 + part
            deeper = jnp.zeros((1, degrees), jnp.float32)
            for other in range(floors):
                value = sum_recv[other, at : at + 1, :]
                deeper = deeper + jnp.where(other > floor, value, 0.0)
            first = (part * fields + 2) * layers
            geo[slot, first : first + layers, :] += deeper
    for copy in home:
        copy.wait()
    pieces = [piece.astype(jnp.float32) for piece in joined_rows(dims, back)]
    joined = jnp.concatenate(pieces, 0).astype(jnp.bfloat16)
    for slot, value in enumerate(final_stage(dims, joined, leg, perm_ref)):
        out_ref[slot] = ((value + geo[slot]) * live[slot]).astype(jnp.bfloat16)


def body(spec, legendre, layer_depth_share, quad_weight, wave_of_slot):
    slots, columns, degrees = spec.shape
    total_lat = legendre.shape[1]
    groups = lax.axis_size("wave")
    layers = layer_depth_share.shape[0]
    quarter = total_lat // groups // 4
    depth = 2 * slots * groups
    block = max(b for b in range(1, quarter + 1) if quarter % b == 0 and b * depth <= max(256, depth))
    dims = dict(
        slots=slots, columns=columns, half=total_lat // 2, groups=groups, layers=layers,
        fields=columns // (2 * layers), quarter=quarter, block=block, waves=slots * groups,
    )
    fields = dims["fields"]
    maps = lane_maps(slots, fields, layers)
    perm = np.zeros((LANES, LANES), np.float32)
    perm[maps, np.arange(LANES)] = 1.0
    perm = jnp.asarray(perm, jnp.bfloat16)
    lat = np.arange(total_lat)
    coriolis = jnp.asarray(2.0 * np.cos(np.pi * (lat + 0.5) / total_lat), jnp.float32)
    floors = lax.axis_size("lev")
    half, count = total_lat // 2, 2 * quarter
    vmem = pl.BlockSpec(memory_space=pltpu.VMEM)
    smem = pl.BlockSpec(memory_space=pltpu.SMEM)
    rows = pltpu.VMEM((groups, count, LANES), jnp.bfloat16)
    flat = pltpu.VMEM((groups * count, LANES), jnp.float32)
    sums = 2 * slots
    return pl.pallas_call(
        functools.partial(whole_kernel, dims),
        out_shape=jax.ShapeDtypeStruct(spec.shape, jnp.bfloat16),
        in_specs=[vmem, pl.BlockSpec(memory_space=pl.ANY), vmem] + [smem] * 4,
        out_specs=vmem,
        scratch_shapes=[
            pltpu.VMEM(legendre.shape, jnp.bfloat16),
            pltpu.VMEM((half, LANES), jnp.float32),
            rows, rows, rows, rows,
            pltpu.VMEM((8, LANES), jnp.float32),
            pltpu.VMEM((groups * 8, LANES), jnp.float32),
            pltpu.VMEM((sums, degrees), jnp.float32),
            pltpu.VMEM((floors, sums, degrees), jnp.float32),
            pltpu.VMEM(spec.shape, jnp.float32),
            flat, flat, flat,
            pltpu.SemaphoreType.DMA((2 * slots,)),
            pltpu.SemaphoreType.DMA((groups,)),
            pltpu.SemaphoreType.DMA((groups,)),
            pltpu.SemaphoreType.DMA((floors,)),
            pltpu.SemaphoreType.DMA((floors,)),
            pltpu.SemaphoreType.DMA((groups,)),
            pltpu.SemaphoreType.DMA((groups,)),
            pltpu.SemaphoreType.DMA((groups,)),
            pltpu.SemaphoreType.DMA((groups,)),
        ]
        + grid_scratch(dims),
        compiler_params=pltpu.CompilerParams(collective_id=0, has_side_effects=True),
    )(spec, legendre, perm, layer_depth_share, quad_weight, coriolis, wave_of_slot)


def solution(mesh):
    in_specs = (P("wave", "lev", None), P("wave", None, None), P("lev"), P(), P("wave"))
    out_specs = P("wave", "lev", None)
    return jax.shard_map(body, mesh=mesh, in_specs=in_specs, out_specs=out_specs, check_vma=False)
```

profile of v0, /device:TPU:0, one launch (start us, length us, event | category | flops | bytes accessed | tf_op | source)
XLA Modules:
  0.0 28.6 jit_solution(1437719395267830336)
XLA Ops:
  0.0 27.0 %shard_map.73 = bf16[2,32,640]{2,1,0:T(8,128)(2,1)} custom-call(bf16[2,32,640]{2,1,0:T(8,128)(2,1)} %spec_ref.1, bf16[2,1280,640]{2,1,0:T(8,128)(2,1)} %leg_hbm.1, bf16[128,128]{1,0:T(8,128)(2,1)} %constant.4.clone.perm_ref, f32[4]{0:T(128)} %share_ref.1, f32[1280]{0:T(1024)} %quad_ref.1, f32[1280]{0:T(1024)} %constant.5.clone.cor_ref, s32[2]{0:T(128)} %wave_ref.1), custom_call_target="tpu_custom_call" | custom-call | tf_op jit(solution)/shard_map/pallas_call | solution.py:542
  27.0 1.5 %copy.9 = bf16[2,32,640]{2,1,0:T(8,128)(2,1)} copy(bf16[2,32,640]{2,1,0:T(8,128)(2,1)} %shard_map.73) | data formatting | bytes 163840
where the time goes:
time: 28.8 us; the launch traced here: 28.6 us
  Pallas kernels  27 us (94%)
  local copies, waits for them, and re-layouts  1.53 us (5%)
    pallas_call x1, Pallas kernels, body(): pl.pallas_call(functools.partial(whole_kernel, dims), out_shape=jax.Shape...  27 us
    unnamed x1, local copies, waits for them, and re-layouts  1.53 us

commit v1 on v0

--- a/solution.py
+++ b/solution.py
@@ -11,7 +11,8 @@
 
 LANES = 128
 POINTS = 2 * LANES
-UNROLL = 4
+UNROLL = 16
+VMEM_BYTES = 48 * 2**20
 NT = (((1,), (1,)), ((), ()))
 
 
@@ -405,16 +406,27 @@
 
 
 def whole_kernel(
-    dims, spec_ref, leg_hbm, perm_ref, share_ref, quad_ref, cor_ref, wave_ref, out_ref,
+    dims, spec_hbm, leg_hbm, perm_hbm, share_hbm, quad_hbm, cor_hbm, wave_hbm, out_ref,
+    spec_ref, perm_ref, share_ref, quad_ref, cor_ref, wave_ref, in_sem,
     leg, rows, send, recv, back_send, back, wave_send, wave_recv, sum_send, sum_recv, geo,
     get, north, south, load_sem, sem_a, sem_b, sem_c, sem_d, sem_e, sem_f, sem_g, sem_h, *scratch,
 ):
     slots, groups, half = dims["slots"], dims["groups"], dims["half"]
     fields, layers, count = dims["fields"], dims["layers"], 2 * dims["quarter"]
-    degrees = spec_ref.shape[2]
+    degrees = spec_hbm.shape[2]
     me = lax.axis_index("wave")
     floor = lax.axis_index("lev")
     floors = lax.axis_size("lev")
+    pairs = (
+        (spec_hbm, spec_ref), (wave_hbm, wave_ref), (share_hbm, share_ref),
+        (perm_hbm, perm_ref), (quad_hbm, quad_ref), (cor_hbm, cor_ref),
+    )
+    brought = [
+        pltpu.make_async_copy(source, target, in_sem.at[k])
+        for k, (source, target) in enumerate(pairs)
+    ]
+    for copy in brought:
+        copy.start()
     loads = []
     for slot in range(slots):
         for hemi in range(2):
@@ -430,6 +442,8 @@
             pl.semaphore_signal(
                 barrier, inc=1, device_id=to_peer(axis, shift), device_id_type=pl.DeviceIdType.MESH
             )
+    for copy in brought:
+        copy.wait()
     degree = lax.broadcasted_iota(jnp.int32, (1, degrees), 1)
     live = [
         jnp.where(degree < degrees - wave_ref[slot], 1.0, 0.0).astype(jnp.float32)
@@ -535,16 +549,24 @@
     floors = lax.axis_size("lev")
     half, count = total_lat // 2, 2 * quarter
     vmem = pl.BlockSpec(memory_space=pltpu.VMEM)
-    smem = pl.BlockSpec(memory_space=pltpu.SMEM)
     rows = pltpu.VMEM((groups, count, LANES), jnp.bfloat16)
     flat = pltpu.VMEM((groups * count, LANES), jnp.float32)
     sums = 2 * slots
+    operands = (spec, legendre, perm, layer_depth_share, quad_weight, coriolis, wave_of_slot)
+    operands = [pltpu.with_memory_space_constraint(x, pltpu.HBM) for x in operands]
     return pl.pallas_call(
         functools.partial(whole_kernel, dims),
         out_shape=jax.ShapeDtypeStruct(spec.shape, jnp.bfloat16),
-        in_specs=[vmem, pl.BlockSpec(memory_space=pl.ANY), vmem] + [smem] * 4,
+        in_specs=[pl.BlockSpec(memory_space=pltpu.HBM)] * len(operands),
         out_specs=vmem,
         scratch_shapes=[
+            pltpu.VMEM(spec.shape, jnp.bfloat16),
+            pltpu.VMEM((LANES, LANES), jnp.bfloat16),
+            pltpu.SMEM(layer_depth_share.shape, jnp.float32),
+            pltpu.SMEM(quad_weight.shape, jnp.float32),
+            pltpu.SMEM(quad_weight.shape, jnp.float32),
+            pltpu.SMEM(wave_of_slot.shape, jnp.int32),
+            pltpu.SemaphoreType.DMA((6,)),
             pltpu.VMEM(legendre.shape, jnp.bfloat16),
             pltpu.VMEM((half, LANES), jnp.float32),
             rows, rows, rows, rows,
@@ -565,8 +587,8 @@
             pltpu.SemaphoreType.DMA((groups,)),
         ]
         + grid_scratch(dims),
-        compiler_params=pltpu.CompilerParams(collective_id=0, has_side_effects=True),
-    )(spec, legendre, perm, layer_depth_share, quad_weight, coriolis, wave_of_slot)
+        compiler_params=pltpu.CompilerParams(collective_id=0, has_side_effects=True, vmem_limit_bytes=VMEM_BYTES),
+    )(*operands)
 
 
 def solution(mesh):

time: 28.8 us -> 24.6 us (0.85)
  Pallas kernels: 27 us -> 23.8 us
  local copies, waits for them, and re-layouts: 1.53 us -> 0.64 us
    pallas_call x1, Pallas kernels: 27 us -> 23.8 us  [body(): pl.pallas_call(functools.partial(whole_kernel, dims), out_shape=jax.Shape...]
    unnamed x1, local copies, waits for them, and re-layouts: 1.53 us -> 0.64 us
where the time goes in v1:
time: 24.6 us; the launch traced here: 24.5 us
  Pallas kernels  23.8 us (97%)
  local copies, waits for them, and re-layouts  0.64 us (3%)
    pallas_call x1, Pallas kernels, body(): pl.pallas_call(functools.partial(whole_kernel, dims), out_shape=jax.Shape...  23.8 us
    unnamed x1, local copies, waits for them, and re-layouts  0.64 us

profile of v1, /device:TPU:0, one launch (start us, length us, event | category | flops | bytes accessed | tf_op | source)
XLA Modules:
  0.0 24.5 jit_solution(17058627593086795502)
XLA Ops:
  0.0 23.8 %shard_map.73 = bf16[2,32,640]{2,1,0:T(8,128)(2,1)S(1)} custom-call(bf16[2,32,640]{2,1,0:T(8,128)(2,1)} %spec_hbm.1, bf16[2,1280,640]{2,1,0:T(8,128)(2,1)} %leg_hbm.1, bf16[128,128]{1,0:T(8,128)(2,1)} %constant.4.clone.perm_hbm, f32[4]{0:T(128)} %share_hbm.1, f32[1280]{0:T(1024)} %quad_hbm.1, f32[1280]{0:T(1024)} %constant.5.clone.cor_hbm, s32[2]{0:T(128)} %wave_hbm.1), custom_call_target="tpu_custom_call" | custom-call | tf_op jit(solution)/shard_map/pallas_call | solution.py:557
  23.8 0.6 %copy.9 = bf16[2,32,640]{2,1,0:T(8,128)(2,1)} copy(bf16[2,32,640]{2,1,0:T(8,128)(2,1)S(1)} %shard_map.73) | data formatting | bytes 163840

commit v2 on v1

--- a/solution.py
+++ b/solution.py
@@ -12,6 +12,7 @@
 LANES = 128
 POINTS = 2 * LANES
 UNROLL = 16
+FILLS = 4
 VMEM_BYTES = 48 * 2**20
 NT = (((1,), (1,)), ((), ()))
 
@@ -29,9 +30,11 @@
 
 def turn_trig(steps, length, inverse):
     whole = jnp.floor(steps * inverse + 0.5)
-    angle = (steps - whole * length) * inverse * (2.0 * math.pi)
+    angle = (steps - whole * length) * (inverse * math.pi)
     square = angle * angle
-    return horner(square, taylor(0, 10)), angle * horner(square, taylor(1, 10))
+    sine = angle * horner(square, taylor(1, 6))
+    twice = sine + sine
+    return 1.0 - twice * sine, twice * horner(square, taylor(0, 7))
 
 
 def lane_maps(slots, fields, layers):
@@ -112,14 +115,25 @@
     return u // share * LANES + inner * dims["groups"]
 
 
-def table_stage(dims, device, waves, quad_ref, cor_ref, scratch):
-    slots, groups, half = dims["slots"], dims["groups"], dims["half"]
-    fields, layers, block = dims["fields"], dims["layers"], dims["block"]
-    state, hop, tab, back_tab, cor, scale = scratch
-    total_lat = 2 * half
-    pair = min(2, block)
-    wide = slots * block * groups
-    lane = lax.broadcasted_iota(jnp.int32, (groups, LANES), 1).astype(jnp.float32)
+def lane_middle(value):
+    return jnp.broadcast_to(value[:, LANES // 2 : LANES // 2 + 1], value.shape)
+
+
+def prepare_stage(dims, device, degrees, quad_ref, cor_ref, partner, cor, scale):
+    groups, half, quarter = dims["groups"], dims["half"], dims["quarter"]
+    layers, block = dims["layers"], dims["block"]
+    total_lat, count = 2 * half, 2 * quarter
+    row = lax.broadcasted_iota(jnp.int32, (count, LANES), 0)
+    dist = row + jnp.where(row < quarter, device * quarter, half - (device + 2) * quarter)
+    length = (20 + 4 * dist).astype(jnp.float32)
+    inverse = 1.0 / length
+    lane = lax.broadcasted_iota(jnp.int32, (count, LANES), 1)
+    cosine, sine = turn_trig(((degrees - 1) * lane).astype(jnp.float32), length, inverse)
+    mid_cos, mid_sin = lane_middle(cosine), lane_middle(sine)
+    partner[0], partner[1] = cosine, sine
+    partner[2] = mid_cos * mid_cos - mid_sin * mid_sin
+    partner[3] = 2.0 * mid_cos * mid_sin
+    partner[4] = inverse
     north_row = lax.broadcasted_iota(jnp.int32, (2 * layers, LANES), 0) < layers
     wave_row = lax.broadcasted_iota(jnp.int32, (2 * layers, POINTS), 0) < layers
     width = 2 * dims["waves"]
@@ -130,57 +144,125 @@
         share = LANES // width
         owner = column // LANES * share + column // groups % share
 
-    def group(number, first):
-        local, dist, lengths, floats = whereabouts(dims, device, number)
+    def group(number, carry):
+        _, dist, _, floats = whereabouts(dims, device, number)
         scaled = jnp.zeros((2 * layers, POINTS), jnp.float32)
         for u, length in enumerate(floats):
-            inverse = 1.0 / jnp.full((groups, LANES), length, jnp.float32)
-            for slot in range(slots):
-                begin = turn_trig(waves[slot] * lane, length, inverse)
-                cosine = jnp.broadcast_to(begin[0][:, LANES // 2 : LANES // 2 + 1], (groups, LANES))
-                sine = jnp.broadcast_to(begin[1][:, LANES // 2 : LANES // 2 + 1], (groups, LANES))
-                keep = jnp.where(2.0 * waves[slot] < length, 1.0, 0.0)
-                at = (slot * block + u) * groups
-                state[0, at : at + groups, :] = begin[0] * keep
-                state[1, at : at + groups, :] = begin[1] * keep
-                hop[0, at : at + groups, :] = cosine * cosine - sine * sine
-                hop[1, at : at + groups, :] = 2.0 * cosine * sine
             cor[number, u * 2 * layers : (u + 1) * 2 * layers, :] = jnp.where(
                 north_row, cor_ref[dist[u]], cor_ref[total_lat - 1 - dist[u]]
             )
             here = jnp.where(wave_row, quad_ref[dist[u]], quad_ref[total_lat - 1 - dist[u]])
             scaled = jnp.where(owner == u, here / length, scaled)
         scale[number] = scaled
-
-        def tile(index, item):
-            for side in range(POINTS // LANES):
-                cols = slice(side * LANES, (side + 1) * LANES)
-                point = lane + (index * POINTS + side * LANES).astype(jnp.float32)
-                start = jnp.minimum(point + 0.5, 1.0)
-                weight = [
-                    jnp.maximum(jnp.minimum(0.5 * length + 0.5 - point, start), 0.0)
-                    for length in floats
+        return carry
+
+    lax.fori_loop(0, count // block, group, 0)
+
+
+def base_stage(dims, device, waves, partner, state, hop):
+    groups, block = dims["groups"], dims["block"]
+    lane = lax.broadcasted_iota(jnp.int32, (groups, LANES), 1).astype(jnp.float32)
+    number = 2 * dims["quarter"] // block
+    pace = 2 if number % 2 == 0 else 1
+
+    def group(step, carry):
+        for n in [step * pace + k for k in range(pace)]:
+            floats = whereabouts(dims, device, n)[3]
+            for u, length in enumerate(floats):
+                full_cos, full_sin, jump_cos, jump_sin, inverse = [
+                    jnp.broadcast_to(partner[k, pl.ds(n * block + u, 1), :], (groups, LANES))
+                    for k in range(5)
                 ]
-                for u in range(0, block, pair):
-                    both = jnp.concatenate(weight[u : u + pair], 0).astype(jnp.bfloat16)
-                    for slot in range(slots):
-                        at = (slot * block + u) * groups
-                        rows = slice(at, at + pair * groups)
-                        cosine, sine = state[0, rows, :], state[1, rows, :]
-                        turn_cos, turn_sin = hop[0, rows, :], hop[1, rows, :]
-                        state[0, rows, :] = cosine * turn_cos - sine * turn_sin
-                        state[1, rows, :] = sine * turn_cos + cosine * turn_sin
-                        for part, value in enumerate((cosine, sine)):
-                            packed = value.astype(jnp.bfloat16)
-                            put = part * wide + at
-                            tab[item, put : put + pair * groups, cols] = packed
-                            put = back_home(dims, part, slot, u)
-                            back_tab[item, put : put + pair * groups, cols] = packed * both
-            return item + 1
-
-        return lax.fori_loop(0, tiles_of(lengths[-1]), tile, first)
-
-    lax.fori_loop(0, 2 * dims["quarter"] // block, group, 0)
+                cosine, sine = turn_trig(waves[0] * lane, length, inverse)
+                mid_cos, mid_sin = lane_middle(cosine), lane_middle(sine)
+                turn_cos = mid_cos * mid_cos - mid_sin * mid_sin
+                turn_sin = 2.0 * mid_cos * mid_sin
+                keep = [jnp.where(2.0 * wave < length, 1.0, 0.0) for wave in waves]
+                rows = slice(u * groups, (u + 1) * groups)
+                state[n, 0, rows, :] = cosine * keep[0]
+                state[n, 1, rows, :] = sine * keep[0]
+                hop[n, 0, rows, :] = turn_cos
+                hop[n, 1, rows, :] = turn_sin
+                rows = slice((block + u) * groups, (block + u + 1) * groups)
+                state[n, 0, rows, :] = (full_cos * cosine + full_sin * sine) * keep[1]
+                state[n, 1, rows, :] = (full_sin * cosine - full_cos * sine) * keep[1]
+                hop[n, 0, rows, :] = jump_cos * turn_cos + jump_sin * turn_sin
+                hop[n, 1, rows, :] = jump_sin * turn_cos - jump_cos * turn_sin
+        return carry
+
+    lax.fori_loop(0, number // pace, group, 0)
+
+
+def tile_list(dims, device):
+    sizes = [
+        tiles_of(whereabouts(dims, device, n)[2][-1])
+        for n in range(2 * dims["quarter"] // dims["block"])
+    ]
+    ends = []
+    for size in sizes:
+        ends.append(size + (ends[-1] if ends else 0))
+    return sizes, ends
+
+
+def tile_at(tiles, item):
+    number, start = 0, 0
+    for size, end in zip(*tiles):
+        number = number + jnp.where(item >= end, 1, 0)
+        start = start + jnp.where(item >= end, size, 0)
+    return number, item - start
+
+
+def fill_tile(dims, device, tiles, item, place, state, hop, tab, back_tab):
+    slots, groups, block = dims["slots"], dims["groups"], dims["block"]
+    pair = min(2, block)
+    wide = slots * block * groups
+    sides = POINTS // LANES
+    number, index = tile_at(tiles, item)
+    length = whereabouts(dims, device, number)[3][0]
+    lane = lax.broadcasted_iota(jnp.int32, (groups, LANES), 1).astype(jnp.float32)
+    weight = []
+    for side in range(sides):
+        point = lane + (index * POINTS + side * LANES).astype(jnp.float32)
+        start = jnp.minimum(point + 0.5, 1.0)
+        reach = (0.5 * length + 0.5) - point
+        each = [jnp.maximum(jnp.minimum(reach + 2.0 * u, start), 0.0) for u in range(block)]
+        weight.append(
+            [
+                jnp.concatenate(each[u : u + pair], 0).astype(jnp.bfloat16)
+                for u in range(0, block, pair)
+            ]
+        )
+    for u in range(0, block, pair):
+        for slot in range(slots):
+            at = (slot * block + u) * groups
+            rows = slice(at, at + pair * groups)
+            cosine, sine = state[number, 0, rows, :], state[number, 1, rows, :]
+            turn_cos, turn_sin = hop[number, 0, rows, :], hop[number, 1, rows, :]
+            for side in range(sides):
+                for part, value in enumerate((cosine, sine)):
+                    packed = value.astype(jnp.bfloat16)
+                    put = part * wide + at
+                    tab[place, side, put : put + pair * groups, :] = packed
+                    put = back_home(dims, part, slot, u)
+                    back_tab[place, side, put : put + pair * groups, :] = (
+                        packed * weight[side][u // pair]
+                    )
+                cosine, sine = (
+                    cosine * turn_cos - sine * turn_sin,
+                    sine * turn_cos + cosine * turn_sin,
+                )
+            state[number, 0, rows, :] = cosine
+            state[number, 1, rows, :] = sine
+
+
+def fill_stage(dims, device, tiles, state, hop, tab, back_tab):
+    def body(step, carry):
+        for k in range(FILLS):
+            item = step * FILLS + k
+            fill_tile(dims, device, tiles, item, item, state, hop, tab, back_tab)
+        return carry
+
+    lax.fori_loop(0, (tiles[1][-1] + FILLS - 1) // FILLS, body, 0)
 
 
 def coefficient_stage(dims, get_ref, base, total):
@@ -190,7 +272,9 @@
     number = count // block
     lane = lax.broadcasted_iota(jnp.int32, (groups, LANES), 1)
     south_lane = lane // layers % 2 == 1
-    first_slot = lax.broadcasted_iota(jnp.int32, (width, LANES), 1) < block * groups
+    owner = lax.broadcasted_iota(jnp.int32, (width, LANES), 1)
+    first_slot = owner < block * groups
+    owner = owner // groups % block
     eye = (
         lax.broadcasted_iota(jnp.int32, (LANES, LANES), 0)
         == lax.broadcasted_iota(jnp.int32, (LANES, LANES), 1)
@@ -212,51 +296,41 @@
             preferred_element_type=jnp.float32,
         )
         for n in range(start, min(start + 2, number)):
-            mine = turned[:, (n - start) * LANES : (n - start + 1) * LANES]
+            here = turned[:, (n - start) * LANES : (n - start + 1) * LANES]
             for part in range(2):
                 value = [
-                    mine[(slot * 2 + part) * width : (slot * 2 + part + 1) * width]
+                    here[(slot * 2 + part) * width : (slot * 2 + part + 1) * width]
                     for slot in range(slots)
                 ]
-                base[n, :, part * LANES : (part + 1) * LANES] = jnp.where(
-                    first_slot, value[0], value[1]
-                ).astype(jnp.bfloat16)
+                value = jnp.where(first_slot, value[0], value[1])
+                for u in range(block):
+                    mine = jnp.where(owner == u, value, 0.0)
+                    near = (-mine if part else mine).astype(jnp.bfloat16)
+                    base[n, part, u * 2 * width : (u * 2 + 1) * width, :] = near
+                    far = mine.astype(jnp.bfloat16)
+                    base[n, part, (u * 2 + 1) * width : (u * 2 + 2) * width, :] = far
     total[...] = jnp.zeros_like(total)
 
 
-def item_stage(dims, device, base, tab, back_tab, cor, total):
+def side_by_side(ref, index):
+    return jnp.concatenate([ref[index, side] for side in range(ref.shape[1])], 1)
+
+
+def item_stage(dims, device, tiles, state, hop, base, tab, back_tab, cor, total):
     groups, layers, block = dims["groups"], dims["layers"], dims["block"]
-    fields, number = dims["fields"], 2 * dims["quarter"] // dims["block"]
+    fields = dims["fields"]
     width = fields * 2 * layers
     rows = 2 * width
-    ends = []
-    for n in range(number):
-        lengths = whereabouts(dims, device, n)[2]
-        ends.append(tiles_of(lengths[-1]) + (ends[-1] if ends else 0))
-    lane = lax.broadcasted_iota(jnp.int32, (width, LANES), 1)
-    mine = [
-        (lane // groups % block == u).astype(jnp.float32).astype(jnp.bfloat16)
-        for u in range(block)
-    ]
     span = 2 * dims["waves"]
     share = max(1, LANES // span)
     reach = max(LANES, span)
     across = lax.broadcasted_iota(jnp.int32, (width, reach), 1)
     sign = jnp.where(across // (reach // 2) == 0, 1.0, -1.0)
 
-    def one(item):
-        n = 0
-        for end in ends:
-            n = n + jnp.where(item >= end, 1, 0)
-        real = base[n, :, :LANES]
-        imag = base[n, :, LANES:]
-        pieces = []
-        for u in range(block):
-            left, right = real * mine[u], imag * mine[u]
-            pieces.append(jnp.concatenate([left, -right], 1))
-            pieces.append(jnp.concatenate([left, right], 1))
+    def one(item, place):
+        n = tile_at(tiles, item)[0]
         grid = jnp.dot(
-            jnp.concatenate(pieces, 0), tab[item], preferred_element_type=jnp.float32
+            side_by_side(base, n), side_by_side(tab, place), preferred_element_type=jnp.float32
         )
         made = []
         for u in range(block):
@@ -276,7 +350,7 @@
                 ]
         products = jnp.concatenate(made, 0).astype(jnp.bfloat16)
         back = lax.dot_general(
-            products, back_tab[item], NT, preferred_element_type=jnp.float32
+            products, side_by_side(back_tab, place), NT, preferred_element_type=jnp.float32
         )
         for start in range(0, block, share):
             column = start * span // LANES * LANES
@@ -291,10 +365,11 @@
 
     def body(step, carry):
         for k in range(UNROLL):
-            one(step * UNROLL + k)
+            item = step * UNROLL + k
+            one(item, item)
         return carry
 
-    lax.fori_loop(0, (ends[-1] + UNROLL - 1) // UNROLL, body, 0)
+    lax.fori_loop(0, (tiles[1][-1] + UNROLL - 1) // UNROLL, body, 0)
 
 
 def return_stage(dims, total, scale, put_refs):
@@ -340,16 +415,17 @@
     layers, fields = dims["layers"], dims["fields"]
     number = 2 * dims["quarter"] // block
     wide = slots * block * groups
+    width = fields * 2 * layers
     items = -(-most_tiles(dims) // UNROLL) * UNROLL
-    width = fields * 2 * layers
     return [
-        pltpu.VMEM((2, wide, LANES), jnp.float32),
-        pltpu.VMEM((2, wide, LANES), jnp.float32),
-        pltpu.VMEM((items, 2 * wide, POINTS), jnp.bfloat16),
-        pltpu.VMEM((items, 2 * wide, POINTS), jnp.bfloat16),
+        pltpu.VMEM((5, number * block, LANES), jnp.float32),
+        pltpu.VMEM((number + 1, 2, wide, LANES), jnp.float32),
+        pltpu.VMEM((number + 1, 2, wide, LANES), jnp.float32),
+        pltpu.VMEM((items, POINTS // LANES, 2 * wide, LANES), jnp.bfloat16),
+        pltpu.VMEM((items, POINTS // LANES, 2 * wide, LANES), jnp.bfloat16),
         pltpu.VMEM((number + 1, block * 2 * layers, LANES), jnp.float32),
         pltpu.VMEM((number, 2 * layers, POINTS), jnp.float32),
-        pltpu.VMEM((number + 1, width, 2 * wide), jnp.bfloat16),
+        pltpu.VMEM((number + 1, 2, block * 2 * width, wide), jnp.bfloat16),
         pltpu.VMEM((number + 1, width, 2 * wide), jnp.float32),
     ]
 
@@ -437,11 +513,17 @@
             copy.start()
             loads.append(copy)
     barrier = pltpu.get_barrier_semaphore()
-    for axis, size in (("wave", groups), ("lev", floors)):
-        for shift in range(1, size):
-            pl.semaphore_signal(
-                barrier, inc=1, device_id=to_peer(axis, shift), device_id_type=pl.DeviceIdType.MESH
-            )
+    for shift in range(1, groups):
+        pl.semaphore_signal(
+            barrier, inc=1, device_id=to_peer("wave", shift), device_id_type=pl.DeviceIdType.MESH
+        )
+
+    @pl.when(floor < floors - 1)
+    def _():
+        pl.semaphore_signal(
+            barrier, inc=1, device_id={"lev": floor + 1}, device_id_type=pl.DeviceIdType.MESH
+        )
+
     for copy in brought:
         copy.wait()
     degree = lax.broadcasted_iota(jnp.int32, (1, degrees), 1)
@@ -474,31 +556,62 @@
         gain = jnp.where(place == slot, twice, gain)
     fourier_stage(dims, spec_ref, leg, loads, live, gain, perm_ref, rows)
     split_rows(dims, rows, send)
-    pl.semaphore_wait(barrier, groups - 1 + floors - 1)
+    pl.semaphore_wait(barrier, groups - 1 + jnp.where(floor > 0, 1, 0))
 
     def wave_place(device):
         return wave_recv.at[pl.ds(pl.multiple_of(device * 8, 8), 8)]
 
     tell = exchange("wave", lambda _: wave_send, wave_place, (sem_a, sem_b))
-    lift = exchange("lev", lambda _: sum_send, lambda p: sum_recv.at[p], (sem_c, sem_d))
+    lift = [
+        pltpu.make_async_remote_copy(
+            src_ref=sum_recv.at[step - 1] if step else sum_send,
+            dst_ref=sum_recv.at[step],
+            send_sem=sem_c.at[step],
+            recv_sem=sem_d.at[step],
+            device_id={"lev": lax.rem(floor + floors - 1, floors)},
+            device_id_type=pl.DeviceIdType.MESH,
+        )
+        for step in range(floors - 1)
+    ]
+
+    def raise_sums(step):
+        if step:
+
+            @pl.when(floor + step < floors)
+            def _():
+                lift[step - 1].wait_recv()
+
+        if step < floors - 1:
+
+            @pl.when((floor > 0) & (floor + step < floors))
+            def _():
+                lift[step].start()
+
     for copy in tell:
         copy.start()
     wave_recv[pl.ds(pl.multiple_of(me * 8, 8), 8), :] = own
     there = exchange("wave", lambda p: send.at[p], lambda p: recv.at[p], (sem_e, sem_f))
-    for copy in there + lift:
+    for copy in there:
         copy.start()
+    raise_sums(0)
     recv[me] = send[me]
+    partner, state, hop, tab, back_tab, cor, scale, base, total = scratch
+    prepare_stage(dims, me, degrees, quad_ref, cor_ref, partner, cor, scale)
+    tiles = tile_list(dims, me)
     for copy in tell:
         copy.wait()
     waves = [wave_recv[pl.ds(slot, groups, stride=8), :] for slot in range(slots)]
-    state, hop, tab, back_tab, cor, scale, base, total = scratch
-    table_stage(dims, me, waves, quad_ref, cor_ref, scratch[:6])
+    base_stage(dims, me, waves, partner, state, hop)
+    raise_sums(1)
+    fill_stage(dims, me, tiles, state, hop, tab, back_tab)
     for copy in there:
         copy.wait()
     for source in range(groups):
         get[source * count : (source + 1) * count, :] = recv[source].astype(jnp.float32)
     coefficient_stage(dims, get, base, total)
-    item_stage(dims, me, base, tab, back_tab, cor, total)
+    if floors > 2:
+        raise_sums(2)
+    item_stage(dims, me, tiles, state, hop, base, tab, back_tab, cor, total)
     return_stage(dims, total, scale, (north, south))
     hemi = lax.broadcasted_iota(jnp.int32, (count, LANES), 1) // layers % 2
     for source in range(groups):
@@ -508,15 +621,21 @@
     for copy in home:
         copy.start()
     back[me] = back_send[me]
-    for copy in lift:
-        copy.wait()
+    for step in range(3, floors):
+        raise_sums(step)
+    for step in range(floors - 1):
+
+        @pl.when((floor > 0) & (floor + step < floors))
+        def _():
+            lift[step].wait_send()
+
     for slot in range(slots):
         for part in range(2):
             at = slot * 2 + part
             deeper = jnp.zeros((1, degrees), jnp.float32)
-            for other in range(floors):
-                value = sum_recv[other, at : at + 1, :]
-                deeper = deeper + jnp.where(other > floor, value, 0.0)
+            for step in range(floors - 1):
+                value = sum_recv[step, at : at + 1, :]
+                deeper = deeper + jnp.where(floor + step + 1 < floors, value, 0.0)
             first = (part * fields + 2) * layers
             geo[slot, first : first + layers, :] += deeper
     for copy in home:

time: 24.6 us -> 23.3 us (0.947)
  Pallas kernels: 23.8 us -> 22.5 us
    pallas_call x1, Pallas kernels: 23.8 us -> 22.5 us  [body(): pl.pallas_call(functools.partial(whole_kernel, dims), out_shape=jax.Shape...]
where the time goes in v2:
time: 23.3 us; the launch traced here: 23.2 us
  Pallas kernels  22.5 us (97%)
  local copies, waits for them, and re-layouts  0.64 us (3%)
    pallas_call x1, Pallas kernels, body(): pl.pallas_call(functools.partial(whole_kernel, dims), out_shape=jax.Shape...  22.5 us
    unnamed x1, local copies, waits for them, and re-layouts  0.64 us

profile of v2, /device:TPU:0, one launch (start us, length us, event | category | flops | bytes accessed | tf_op | source)
XLA Modules:
  0.0 23.2 jit_solution(16289217377750712958)
XLA Ops:
  0.0 22.5 %shard_map.73 = bf16[2,32,640]{2,1,0:T(8,128)(2,1)S(1)} custom-call(bf16[2,32,640]{2,1,0:T(8,128)(2,1)} %spec_hbm.1, bf16[2,1280,640]{2,1,0:T(8,128)(2,1)} %leg_hbm.1, bf16[128,128]{1,0:T(8,128)(2,1)} %constant.4.clone.perm_hbm, f32[4]{0:T(128)} %share_hbm.1, f32[1280]{0:T(1024)} %quad_hbm.1, f32[1280]{0:T(1024)} %constant.5.clone.cor_hbm, s32[2]{0:T(128)} %wave_hbm.1), custom_call_target="tpu_custom_call" | custom-call | tf_op jit(solution)/shard_map/pallas_call | solution.py:676
  22.5 0.6 %copy.9 = bf16[2,32,640]{2,1,0:T(8,128)(2,1)} copy(bf16[2,32,640]{2,1,0:T(8,128)(2,1)S(1)} %shard_map.73) | data formatting | bytes 163840

commit v3 on v2

--- a/solution.py
+++ b/solution.py
@@ -11,7 +11,7 @@
 
 LANES = 128
 POINTS = 2 * LANES
-UNROLL = 16
+UNROLL = 32
 FILLS = 4
 VMEM_BYTES = 48 * 2**20
 NT = (((1,), (1,)), ((), ()))
@@ -43,28 +43,37 @@
     return natural.transpose(0, 2, 3, 1, 4).reshape(-1)
 
 
-def fourier_stage(dims, spec_ref, leg_ref, loads, live, gain, perm_ref, rows_ref):
-    slots, columns, half = dims["slots"], dims["columns"], dims["half"]
-    total = jnp.zeros((half, LANES), jnp.float32)
-    for slot in range(slots):
-        masked = spec_ref[slot] * live[slot].astype(jnp.bfloat16)
-        for hemi in range(2):
-            at = (slot * 2 + hemi) * columns
-            pieces = []
-            if at:
-                pieces.append(jnp.zeros((at, masked.shape[1]), masked.dtype))
-            pieces.append(masked)
-            if at + columns < LANES:
-                pieces.append(jnp.zeros((LANES - at - columns, masked.shape[1]), masked.dtype))
+def spread_rows(dims, hemi, masked):
+    layers = dims["layers"]
+    row = lax.broadcasted_iota(jnp.int32, (2 * layers, masked.shape[1]), 0)
+    keep = row // layers == hemi
+    pieces = []
+    for at in range(0, masked.shape[0], 2 * layers):
+        here = masked[at : at + 2 * layers]
+        turned = pltpu.roll(here, layers, 0)
+        pieces += [turned, here] if hemi else [here, turned]
+    return jnp.concatenate([jnp.where(keep, piece, 0.0) for piece in pieces], 0)
+
+
+def fourier_stage(dims, full, leg_ref, loads, gain, rows_ref):
+    slots, half = dims["slots"], dims["half"]
+    total = 0.0
+    for hemi in range(2):
+        weights = []
+        for slot in range(slots):
+            mine = spread_rows(dims, hemi, full[slot]).astype(jnp.bfloat16)
+            blank = jnp.zeros_like(mine)
+            weights.append(
+                jnp.concatenate([mine if k == slot else blank for k in range(slots)], 1)
+            )
+        weights = jnp.concatenate(weights, 0)
+        for slot in range(slots):
             loads[slot * 2 + hemi].wait()
-            total += lax.dot_general(
-                leg_ref[slot, hemi * half : (hemi + 1) * half, :],
-                jnp.concatenate(pieces, 0),
-                NT,
-                preferred_element_type=jnp.float32,
-            )
-    rows = jnp.dot(total.astype(jnp.bfloat16), perm_ref[...], preferred_element_type=jnp.float32)
-    rows_ref[...] = rows * gain
+        table = [leg_ref[slot, hemi * half : (hemi + 1) * half, :] for slot in range(slots)]
+        total += lax.dot_general(
+            jnp.concatenate(table, 1), weights, NT, preferred_element_type=jnp.float32
+        )
+    rows_ref[...] = total * gain
 
 
 def split_rows(dims, rows_ref, send_ref):
@@ -228,7 +237,7 @@
         each = [jnp.maximum(jnp.minimum(reach + 2.0 * u, start), 0.0) for u in range(block)]
         weight.append(
             [
-                jnp.concatenate(each[u : u + pair], 0).astype(jnp.bfloat16)
+                jnp.concatenate(each[u : u + pair], 0)
                 for u in range(0, block, pair)
             ]
         )
@@ -240,13 +249,12 @@
             turn_cos, turn_sin = hop[number, 0, rows, :], hop[number, 1, rows, :]
             for side in range(sides):
                 for part, value in enumerate((cosine, sine)):
-                    packed = value.astype(jnp.bfloat16)
                     put = part * wide + at
-                    tab[place, side, put : put + pair * groups, :] = packed
+                    tab[place, side, put : put + pair * groups, :] = value.astype(jnp.bfloat16)
                     put = back_home(dims, part, slot, u)
                     back_tab[place, side, put : put + pair * groups, :] = (
-                        packed * weight[side][u // pair]
-                    )
+                        value * weight[side][u // pair]
+                    ).astype(jnp.bfloat16)
                 cosine, sine = (
                     cosine * turn_cos - sine * turn_sin,
                     sine * turn_cos + cosine * turn_sin,
@@ -272,9 +280,7 @@
     number = count // block
     lane = lax.broadcasted_iota(jnp.int32, (groups, LANES), 1)
     south_lane = lane // layers % 2 == 1
-    owner = lax.broadcasted_iota(jnp.int32, (width, LANES), 1)
-    first_slot = owner < block * groups
-    owner = owner // groups % block
+    first_slot = lax.broadcasted_iota(jnp.int32, (width, LANES), 1) < block * groups
     eye = (
         lax.broadcasted_iota(jnp.int32, (LANES, LANES), 0)
         == lax.broadcasted_iota(jnp.int32, (LANES, LANES), 1)
@@ -303,12 +309,7 @@
                     for slot in range(slots)
                 ]
                 value = jnp.where(first_slot, value[0], value[1])
-                for u in range(block):
-                    mine = jnp.where(owner == u, value, 0.0)
-                    near = (-mine if part else mine).astype(jnp.bfloat16)
-                    base[n, part, u * 2 * width : (u * 2 + 1) * width, :] = near
-                    far = mine.astype(jnp.bfloat16)
-                    base[n, part, (u * 2 + 1) * width : (u * 2 + 2) * width, :] = far
+                base[n, part] = value.astype(jnp.bfloat16)
     total[...] = jnp.zeros_like(total)
 
 
@@ -321,6 +322,11 @@
     fields = dims["fields"]
     width = fields * 2 * layers
     rows = 2 * width
+    lane = lax.broadcasted_iota(jnp.int32, (width, LANES), 1)
+    mine = [
+        (lane // groups % block == u).astype(jnp.float32).astype(jnp.bfloat16)
+        for u in range(block)
+    ]
     span = 2 * dims["waves"]
     share = max(1, LANES // span)
     reach = max(LANES, span)
@@ -329,8 +335,15 @@
 
     def one(item, place):
         n = tile_at(tiles, item)[0]
+        pieces = []
+        for u in range(block):
+            left, right = base[n, 0] * mine[u], base[n, 1] * mine[u]
+            pieces.append(jnp.concatenate([left, -right], 1))
+            pieces.append(jnp.concatenate([left, right], 1))
         grid = jnp.dot(
-            side_by_side(base, n), side_by_side(tab, place), preferred_element_type=jnp.float32
+            jnp.concatenate(pieces, 0),
+            side_by_side(tab, place),
+            preferred_element_type=jnp.float32,
         )
         made = []
         for u in range(block):
@@ -425,26 +438,25 @@
         pltpu.VMEM((items, POINTS // LANES, 2 * wide, LANES), jnp.bfloat16),
         pltpu.VMEM((number + 1, block * 2 * layers, LANES), jnp.float32),
         pltpu.VMEM((number, 2 * layers, POINTS), jnp.float32),
-        pltpu.VMEM((number + 1, 2, block * 2 * width, wide), jnp.bfloat16),
+        pltpu.VMEM((number + 1, 2, width, wide), jnp.bfloat16),
         pltpu.VMEM((number + 1, width, 2 * wide), jnp.float32),
     ]
 
 
 def final_stage(dims, get, leg_ref, perm_ref):
-    slots, columns, half = dims["slots"], dims["columns"], dims["half"]
+    slots, columns = dims["slots"], dims["columns"]
     turned = lax.dot_general(
         perm_ref[...], get, NT, preferred_element_type=jnp.float32
     ).astype(jnp.bfloat16)
     results = []
     for slot in range(slots):
-        total = 0.0
-        for hemi in range(2):
-            at = (slot * 2 + hemi) * columns
-            total += jnp.dot(
-                turned[at : at + columns],
-                leg_ref[slot, hemi * half : (hemi + 1) * half, :],
-                preferred_element_type=jnp.float32,
-            )
+        rows = [
+            turned[(slot * 2 + hemi) * columns : (slot * 2 + hemi + 1) * columns]
+            for hemi in range(2)
+        ]
+        total = jnp.dot(
+            jnp.concatenate(rows, 1), leg_ref[slot], preferred_element_type=jnp.float32
+        )
         results.append(total)
     return results
 
@@ -462,30 +474,58 @@
     return {axis: lax.rem(place + shift, count)}
 
 
+def far_first(count):
+    if count & (count - 1):
+        return list(range(1, count))
+    return sorted(range(1, count), key=lambda d: (-bin(d >> 1).count("1"), d))
+
+
+def partner_of(place, count, step):
+    if count & (count - 1):
+        return lax.rem(place + step, count)
+    peer, bit = place, 1
+    while bit < count:
+        if step & bit:
+            peer = peer + bit * (1 - 2 * lax.rem(lax.div(place, bit), 2))
+        bit *= 2
+    return peer
+
+
 def exchange(axis, source_of, target_of, sems):
     place = lax.axis_index(axis)
     count = lax.axis_size(axis)
     copies = []
-    for shift in range(1, count):
-        peer = lax.rem(place + shift, count)
+    for step in far_first(count):
+        peer = partner_of(place, count, step)
         copies.append(
             pltpu.make_async_remote_copy(
                 src_ref=source_of(peer),
                 dst_ref=target_of(place),
-                send_sem=sems[0].at[shift],
-                recv_sem=sems[1].at[shift],
-                device_id=to_peer(axis, shift),
+                send_sem=sems.at[0],
+                recv_sem=sems.at[1],
+                device_id={axis: peer},
                 device_id_type=pl.DeviceIdType.MESH,
             )
         )
     return copies
+
+
+def all_of(axis, source, target, sems):
+    return pltpu.make_async_remote_copy(
+        src_ref=source,
+        dst_ref=target,
+        send_sem=sems.at[0],
+        recv_sem=sems.at[1],
+        device_id=to_peer(axis, 1),
+        device_id_type=pl.DeviceIdType.MESH,
+    )
 
 
 def whole_kernel(
     dims, spec_hbm, leg_hbm, perm_hbm, share_hbm, quad_hbm, cor_hbm, wave_hbm, out_ref,
     spec_ref, perm_ref, share_ref, quad_ref, cor_ref, wave_ref, in_sem,
     leg, rows, send, recv, back_send, back, wave_send, wave_recv, sum_send, sum_recv, geo,
-    get, north, south, load_sem, sem_a, sem_b, sem_c, sem_d, sem_e, sem_f, sem_g, sem_h, *scratch,
+    get, north, south, load_sem, tell_sem, sem_c, sem_d, there_sem, home_sem, *scratch,
 ):
     slots, groups, half = dims["slots"], dims["groups"], dims["half"]
     fields, layers, count = dims["fields"], dims["layers"], 2 * dims["quarter"]
@@ -493,6 +533,21 @@
     me = lax.axis_index("wave")
     floor = lax.axis_index("lev")
     floors = lax.axis_size("lev")
+    barrier = pltpu.get_barrier_semaphore()
+    for step in far_first(groups):
+        pl.semaphore_signal(
+            barrier,
+            inc=1,
+            device_id={"wave": partner_of(me, groups, step)},
+            device_id_type=pl.DeviceIdType.MESH,
+        )
+
+    @pl.when(floor < floors - 1)
+    def _():
+        pl.semaphore_signal(
+            barrier, inc=1, device_id={"lev": floor + 1}, device_id_type=pl.DeviceIdType.MESH
+        )
+
     pairs = (
         (spec_hbm, spec_ref), (wave_hbm, wave_ref), (share_hbm, share_ref),
         (perm_hbm, perm_ref), (quad_hbm, quad_ref), (cor_hbm, cor_ref),
@@ -507,23 +562,14 @@
     for slot in range(slots):
         for hemi in range(2):
             piece = pl.ds(hemi * half, half)
-            copy = pltpu.make_async_copy(
-                leg_hbm.at[slot, piece], leg.at[slot, piece], load_sem.at[slot * 2 + hemi]
+            loads.append(
+                pltpu.make_async_copy(
+                    leg_hbm.at[slot, piece], leg.at[slot, piece], load_sem.at[slot * 2 + hemi]
+                )
             )
-            copy.start()
-            loads.append(copy)
-    barrier = pltpu.get_barrier_semaphore()
-    for shift in range(1, groups):
-        pl.semaphore_signal(
-            barrier, inc=1, device_id=to_peer("wave", shift), device_id_type=pl.DeviceIdType.MESH
-        )
-
-    @pl.when(floor < floors - 1)
-    def _():
-        pl.semaphore_signal(
-            barrier, inc=1, device_id={"lev": floor + 1}, device_id_type=pl.DeviceIdType.MESH
-        )
-
+    for hemi in range(2):
+        for slot in range(slots):
+            loads[slot * 2 + hemi].start()
     for copy in brought:
         copy.wait()
     degree = lax.broadcasted_iota(jnp.int32, (1, degrees), 1)
@@ -537,8 +583,10 @@
         own = jnp.where(row == slot, wave_ref[slot].astype(jnp.float32), own)
     wave_send[...] = own
     geo[...] = jnp.zeros_like(geo)
+    fulls = []
     for slot in range(slots):
         full = spec_ref[slot].astype(jnp.float32) * live[slot]
+        fulls.append(full)
         for part in range(2):
             first = part * fields * layers
             total = jnp.zeros((1, degrees), jnp.float32)
@@ -554,14 +602,14 @@
     for slot in range(slots):
         twice = jnp.where(wave_ref[slot] == 0, 1.0, 2.0)
         gain = jnp.where(place == slot, twice, gain)
-    fourier_stage(dims, spec_ref, leg, loads, live, gain, perm_ref, rows)
+    fourier_stage(dims, fulls, leg, loads, gain, rows)
     split_rows(dims, rows, send)
     pl.semaphore_wait(barrier, groups - 1 + jnp.where(floor > 0, 1, 0))
 
     def wave_place(device):
         return wave_recv.at[pl.ds(pl.multiple_of(device * 8, 8), 8)]
 
-    tell = exchange("wave", lambda _: wave_send, wave_place, (sem_a, sem_b))
+    tell = exchange("wave", lambda _: wave_send, wave_place, tell_sem)
     lift = [
         pltpu.make_async_remote_copy(
             src_ref=sum_recv.at[step - 1] if step else sum_send,
@@ -590,7 +638,7 @@
     for copy in tell:
         copy.start()
     wave_recv[pl.ds(pl.multiple_of(me * 8, 8), 8), :] = own
-    there = exchange("wave", lambda p: send.at[p], lambda p: recv.at[p], (sem_e, sem_f))
+    there = exchange("wave", lambda p: send.at[p], lambda p: recv.at[p], there_sem)
     for copy in there:
         copy.start()
     raise_sums(0)
@@ -598,14 +646,15 @@
     partner, state, hop, tab, back_tab, cor, scale, base, total = scratch
     prepare_stage(dims, me, degrees, quad_ref, cor_ref, partner, cor, scale)
     tiles = tile_list(dims, me)
-    for copy in tell:
-        copy.wait()
+    others = pl.ds(0, groups - 1)
+    several = pl.ds(0, (groups - 1) * 8)
+    told = all_of("wave", wave_recv.at[several], wave_recv.at[several], tell_sem)
+    told.wait()
     waves = [wave_recv[pl.ds(slot, groups, stride=8), :] for slot in range(slots)]
     base_stage(dims, me, waves, partner, state, hop)
     raise_sums(1)
     fill_stage(dims, me, tiles, state, hop, tab, back_tab)
-    for copy in there:
-        copy.wait()
+    all_of("wave", send.at[others], recv.at[others], there_sem).wait()
     for source in range(groups):
         get[source * count : (source + 1) * count, :] = recv[source].astype(jnp.float32)
     coefficient_stage(dims, get, base, total)
@@ -617,7 +666,7 @@
     for source in range(groups):
         piece = slice(source * count, (source + 1) * count)
         back_send[source] = jnp.where(hemi == 1, south[piece], north[piece]).astype(jnp.bfloat16)
-    home = exchange("wave", lambda p: back_send.at[p], lambda p: back.at[p], (sem_g, sem_h))
+    home = exchange("wave", lambda p: back_send.at[p], lambda p: back.at[p], home_sem)
     for copy in home:
         copy.start()
     back[me] = back_send[me]
@@ -638,8 +687,7 @@
                 deeper = deeper + jnp.where(floor + step + 1 < floors, value, 0.0)
             first = (part * fields + 2) * layers
             geo[slot, first : first + layers, :] += deeper
-    for copy in home:
-        copy.wait()
+    all_of("wave", back_send.at[others], back.at[others], home_sem).wait()
     pieces = [piece.astype(jnp.float32) for piece in joined_rows(dims, back)]
     joined = jnp.concatenate(pieces, 0).astype(jnp.bfloat16)
     for slot, value in enumerate(final_stage(dims, joined, leg, perm_ref)):
@@ -696,14 +744,11 @@
             pltpu.VMEM(spec.shape, jnp.float32),
             flat, flat, flat,
             pltpu.SemaphoreType.DMA((2 * slots,)),
-            pltpu.SemaphoreType.DMA((groups,)),
-            pltpu.SemaphoreType.DMA((groups,)),
-            pltpu.SemaphoreType.DMA((floors,)),
-            pltpu.SemaphoreType.DMA((floors,)),
-            pltpu.SemaphoreType.DMA((groups,)),
-            pltpu.SemaphoreType.DMA((groups,)),
-            pltpu.SemaphoreType.DMA((groups,)),
-            pltpu.SemaphoreType.DMA((groups,)),
+            pltpu.SemaphoreType.DMA((2,)),
+            pltpu.SemaphoreType.DMA((floors - 1,)),
+            pltpu.SemaphoreType.DMA((floors - 1,)),
+            pltpu.SemaphoreType.DMA((2,)),
+            pltpu.SemaphoreType.DMA((2,)),
         ]
         + grid_scratch(dims),
         compiler_params=pltpu.CompilerParams(collective_id=0, has_side_effects=True, vmem_limit_bytes=VMEM_BYTES),

time: 23.3 us -> 22.5 us (0.966)
  Pallas kernels: 22.5 us -> 21.7 us
    pallas_call x1, Pallas kernels: 22.5 us -> 21.7 us  [body(): pl.pallas_call(functools.partial(whole_kernel, dims), out_shape=jax.Shape...]
where the time goes in v3:
time: 22.5 us; the launch traced here: 22.4 us
  Pallas kernels  21.7 us (96%)
  local copies, waits for them, and re-layouts  0.64 us (3%)
    pallas_call x1, Pallas kernels, body(): pl.pallas_call(functools.partial(whole_kernel, dims), out_shape=jax.Shape...  21.7 us
    unnamed x1, local copies, waits for them, and re-layouts  0.64 us

profile of v3, /device:TPU:0, one launch (start us, length us, event | category | flops | bytes accessed | tf_op | source)
XLA Modules:
  0.0 22.4 jit_solution(6754478561933892667)
XLA Ops:
  0.0 21.7 %shard_map.73 = bf16[2,32,640]{2,1,0:T(8,128)(2,1)S(1)} custom-call(bf16[2,32,640]{2,1,0:T(8,128)(2,1)} %spec_hbm.1, bf16[2,1280,640]{2,1,0:T(8,128)(2,1)} %leg_hbm.1, bf16[128,128]{1,0:T(8,128)(2,1)} %constant.4.clone.perm_hbm, f32[4]{0:T(128)} %share_hbm.1, f32[1280]{0:T(1024)} %quad_hbm.1, f32[1280]{0:T(1024)} %constant.5.clone.cor_hbm, s32[2]{0:T(128)} %wave_hbm.1), custom_call_target="tpu_custom_call" | custom-call | tf_op jit(solution)/shard_map/pallas_call | solution.py:724
  21.8 0.6 %copy.9 = bf16[2,32,640]{2,1,0:T(8,128)(2,1)} copy(bf16[2,32,640]{2,1,0:T(8,128)(2,1)S(1)} %shard_map.73) | data formatting | bytes 163840

commit v4 on v3

--- a/solution.py
+++ b/solution.py
@@ -12,7 +12,7 @@
 LANES = 128
 POINTS = 2 * LANES
 UNROLL = 32
-FILLS = 4
+FILLS = 8
 VMEM_BYTES = 48 * 2**20
 NT = (((1,), (1,)), ((), ()))
 
@@ -172,7 +172,7 @@
     groups, block = dims["groups"], dims["block"]
     lane = lax.broadcasted_iota(jnp.int32, (groups, LANES), 1).astype(jnp.float32)
     number = 2 * dims["quarter"] // block
-    pace = 2 if number % 2 == 0 else 1
+    pace = 5 if number % 5 == 0 else 1
 
     def group(step, carry):
         for n in [step * pace + k for k in range(pace)]:
@@ -273,7 +273,7 @@
     lax.fori_loop(0, (tiles[1][-1] + FILLS - 1) // FILLS, body, 0)
 
 
-def coefficient_stage(dims, get_ref, base, total):
+def coefficient_stage(dims, get_ref, base):
     slots, groups, layers = dims["slots"], dims["groups"], dims["layers"]
     fields, block, count = dims["fields"], dims["block"], 2 * dims["quarter"]
     width = fields * 2 * layers
@@ -310,7 +310,6 @@
                 ]
                 value = jnp.where(first_slot, value[0], value[1])
                 base[n, part] = value.astype(jnp.bfloat16)
-    total[...] = jnp.zeros_like(total)
 
 
 def side_by_side(ref, index):
@@ -645,6 +644,7 @@
     recv[me] = send[me]
     partner, state, hop, tab, back_tab, cor, scale, base, total = scratch
     prepare_stage(dims, me, degrees, quad_ref, cor_ref, partner, cor, scale)
+    total[...] = jnp.zeros_like(total)
     tiles = tile_list(dims, me)
     others = pl.ds(0, groups - 1)
     several = pl.ds(0, (groups - 1) * 8)
@@ -657,7 +657,7 @@
     all_of("wave", send.at[others], recv.at[others], there_sem).wait()
     for source in range(groups):
         get[source * count : (source + 1) * count, :] = recv[source].astype(jnp.float32)
-    coefficient_stage(dims, get, base, total)
+    coefficient_stage(dims, get, base)
     if floors > 2:
         raise_sums(2)
     item_stage(dims, me, tiles, state, hop, base, tab, back_tab, cor, total)

time: 22.5 us -> 22.2 us (0.987)
  Pallas kernels: 21.7 us -> 21.4 us
    pallas_call x1, Pallas kernels: 21.7 us -> 21.4 us  [body(): pl.pallas_call(functools.partial(whole_kernel, dims), out_shape=jax.Shape...]
where the time goes in v4:
time: 22.2 us; the launch traced here: 22.1 us
  Pallas kernels  21.4 us (96%)
  local copies, waits for them, and re-layouts  0.64 us (3%)
    pallas_call x1, Pallas kernels, body(): pl.pallas_call(functools.partial(whole_kernel, dims), out_shape=jax.Shape...  21.4 us
    unnamed x1, local copies, waits for them, and re-layouts  0.64 us

profile of v4, /device:TPU:0, one launch (start us, length us, event | category | flops | bytes accessed | tf_op | source)
XLA Modules:
  0.0 22.1 jit_solution(4749603108675886441)
XLA Ops:
  0.0 21.4 %shard_map.73 = bf16[2,32,640]{2,1,0:T(8,128)(2,1)S(1)} custom-call(bf16[2,32,640]{2,1,0:T(8,128)(2,1)} %spec_hbm.1, bf16[2,1280,640]{2,1,0:T(8,128)(2,1)} %leg_hbm.1, bf16[128,128]{1,0:T(8,128)(2,1)} %constant.4.clone.perm_hbm, f32[4]{0:T(128)} %share_hbm.1, f32[1280]{0:T(1024)} %quad_hbm.1, f32[1280]{0:T(1024)} %constant.5.clone.cor_hbm, s32[2]{0:T(128)} %wave_hbm.1), custom_call_target="tpu_custom_call" | custom-call | tf_op jit(solution)/shard_map/pallas_call | solution.py:724
  21.4 0.6 %copy.9 = bf16[2,32,640]{2,1,0:T(8,128)(2,1)} copy(bf16[2,32,640]{2,1,0:T(8,128)(2,1)S(1)} %shard_map.73) | data formatting | bytes 163840
